TPU v7x, 32 devices: a whole 2x2x4 slice. The times are simulated.
32 devices in a mesh: img: 8 (over y, x, core), ori: 4 (over z).
Axes of the slice: x: 2, y: 2, z: 4, core: 2. Of those that a mesh axis runs over, the one named last changes fastest.
Arguments:
- images: bfloat16 [4096, 4096], P('img'), may hold values from -6 to 6
- ctf_class: int32 [4096], P('img'), may hold values from 0 to 15
- class_mask: int32 [4096, 8], P('img'), may hold values from 0 to 1, as said below
- precision: float32 [4096], P('img'), may hold values from 0.02 to 0.5
- class_log_prior: float32 [4096, 8], P('img'), may hold values from -6 to 406
- ctf_filters: float32 [16, 4096], replicated, may hold values from -1 to 1
- volume_coef: bfloat16 [8, 16, 2, 4096], P(None, 'img'), may hold values from -6 to 6
- slice_ops: bfloat16 [8, 4096, 64], replicated, may hold values from -0.09375 to 0.09375
- tilt_index: int32 [64], P('ori'), may hold values from 0 to 7
- azimuth_index: int32 [64], P('ori'), may hold values from 0 to 31
Outputs:
- coef_sum: float32 [8, 16, 2, 4096], P(None, 'img')
- log_evidence: float32 [4096], P('img')
- class_posterior: float32 [4096, 8], P('img')
Inputs may be any that keep to these rules, and one draw needn't show every extreme that they name: `class_mask`: every image allows at least one class.
All inputs are finite; a program needn't handle non-finite values.
Results may differ from a plain program's by a relative error of at most 0.024.
The roundings to bfloat16 on the way count: a program that leaves them out, or rounds other values in their place, can miss the bound.
Values may be sent and summed in bfloat16 or wider, within the bound.
No kernel may reach another device: no remote copies, remote signals or barrier semaphores. Data moves between devices by JAX's collectives and lax.ppermute only.
A program may use at most 192 MiB of HBM per device.

v0:
```python
import math
import jax
import jax.numpy as jnp
from jax import lax
from jax.sharding import PartitionSpec as P

ORD = 64
ANG = 128
NAZI = 32
LM = 4096


def synth_table():
    orders = (jnp.arange(ORD) - ORD // 2).astype(jnp.float32)
    angles = jnp.arange(ANG).astype(jnp.float32) * (2.0 * math.pi / ANG)
    phase = orders[:, None] * angles[None, :]
    cosine = jnp.cos(phase)
    sine = jnp.sin(phase)
    upper = jnp.concatenate([cosine, sine], axis=1)
    lower = jnp.concatenate([-sine, cosine], axis=1)
    return (jnp.concatenate([upper, lower], axis=0) * ORD ** (-0.5)).astype(jnp.bfloat16)


def rotated_ops(tilts, azimuths, slice_ops):
    chosen = jnp.take(slice_ops, tilts, axis=0).astype(jnp.float32)
    chosen = jnp.transpose(chosen, (1, 0, 2))
    orders = (jnp.arange(LM) % ORD - ORD // 2).astype(jnp.float32)
    turns = azimuths.astype(jnp.float32) * (2.0 * math.pi / NAZI)
    phase = orders[:, None] * turns[None, :]
    cosine = jnp.cos(phase)[:, :, None]
    sine = jnp.sin(phase)[:, :, None]
    upper = jnp.concatenate([cosine * chosen, -sine * chosen], axis=2)
    lower = jnp.concatenate([sine * chosen, cosine * chosen], axis=2)
    rotator = jnp.concatenate([upper, lower], axis=0)
    return rotator.reshape(2 * LM, -1).astype(jnp.bfloat16)


def synthesize(coefs, rotator, angle_table):
    classes, radial = (coefs.shape[0], coefs.shape[1])
    flat_coef = coefs.reshape(classes * radial, 2 * LM)
    harmonics = jnp.dot(flat_coef, rotator, preferred_element_type=jnp.float32).astype(jnp.bfloat16)
    orients = rotator.shape[1] // (2 * ORD)
    harmonics = (
        harmonics.reshape(classes, radial, orients, 2 * ORD)
        .transpose(2, 0, 1, 3)
        .reshape(-1, 2 * ORD)
    )
    values = jnp.dot(harmonics, angle_table, preferred_element_type=jnp.float32).astype(
        jnp.bfloat16
    )
    return values.reshape(orients * classes, radial * 2 * ANG)


def adjoint(back_proj, rotator, angle_table, radial, classes):
    columns = back_proj.shape[1]
    orients = rotator.shape[1] // (2 * ORD)
    spread = (
        back_proj.reshape(radial, 2 * ANG, columns)
        .transpose(0, 2, 1)
        .reshape(radial * columns, 2 * ANG)
    )
    harmonics = jnp.dot(spread, angle_table.T, preferred_element_type=jnp.float32).astype(
        jnp.bfloat16
    )
    harmonics = harmonics.reshape(radial, orients, classes, 2 * ORD).transpose(2, 0, 1, 3)
    harmonics = harmonics.reshape(classes * radial, orients * 2 * ORD)
    return lax.dot_general(
        harmonics, rotator, (((1,), (1,)), ((), ())), preferred_element_type=jnp.float32
    )


def body(
    images,
    ctf_class,
    class_mask,
    precision,
    class_log_prior,
    ctf_filters,
    volume_coef,
    slice_ops,
    tilt_index,
    azimuth_index,
):
    angle_table = synth_table()
    image_rows = images.shape[0]
    classes = volume_coef.shape[0]
    radial = volume_coef.shape[1]
    orients = tilt_index.shape[0]
    filter_count = ctf_filters.shape[0]
    selector = (ctf_class[:, None] == jnp.arange(filter_count)[None, :]).astype(jnp.float32)
    ctf_rows = jnp.dot(selector, ctf_filters, precision=lax.Precision.HIGHEST)
    filtered = (images.astype(jnp.float32) * ctf_rows).astype(jnp.bfloat16)
    ctf_square = ctf_filters * ctf_filters
    rotator = rotated_ops(tilt_index, azimuth_index, slice_ops)
    coefs = lax.all_gather(volume_coef, "img", axis=1, tiled=True)
    templates = synthesize(coefs, rotator, angle_table)
    part_img = filtered
    correl = lax.dot_general(
        part_img, templates, (((1,), (1,)), ((), ())), preferred_element_type=jnp.float32
    )
    square = templates.astype(jnp.float32)
    square = square * square
    energy = lax.dot_general(
        ctf_square, square, (((1,), (1,)), ((), ())), precision=lax.Precision.HIGHEST
    )
    correl, energy = (correl, energy)
    energy_rows = jnp.dot(selector, energy, precision=lax.Precision.HIGHEST)
    score = precision[:, None] * (correl - 0.5 * energy_rows) + jnp.tile(
        class_log_prior, (1, orients)
    )
    allowed = jnp.tile(class_mask, (1, orients)) > 0
    score = jnp.where(allowed, score, -1e30)
    row_peak = lax.pmax(jnp.max(score, axis=1), "ori")
    exponent = jnp.exp(score - row_peak[:, None])
    local_totals = exponent.reshape(image_rows, orients, classes).sum(axis=1)
    totals = lax.psum(local_totals, "ori")
    norm_sum = totals.sum(axis=1)
    log_evidence = row_peak + jnp.log(norm_sum)
    class_posterior = totals / norm_sum[:, None]
    weights = (exponent / norm_sum[:, None]).astype(jnp.bfloat16)
    part_img = filtered
    summed = lax.psum_scatter(
        lax.dot_general(
            part_img, weights, (((0,), (0,)), ((), ())), preferred_element_type=jnp.float32
        ).astype(jnp.bfloat16),
        "img",
        scatter_dimension=0,
        tiled=True,
    )
    coef_own = adjoint(summed, rotator, angle_table, radial, classes)
    coef_sum = (
        lax.psum(coef_own.astype(jnp.bfloat16), "ori")
        .astype(jnp.float32)
        .reshape(classes, radial, 2, LM)
    )
    return (coef_sum, log_evidence, class_posterior)


def solution(mesh):
    placed = (
        P("img", None),
        P("img"),
        P("img", None),
        P("img"),
        P("img", None),
        P(),
        P(None, "img", None, None),
        P(),
        P("ori"),
        P("ori"),
    )
    return jax.shard_map(
        body,
        mesh=mesh,
        in_specs=placed,
        out_specs=(P(None, "img", None, None), P("img"), P("img", None)),
        check_vma=False,
    )
```

profile of v0, /device:TPU:0, one launch (start us, length us, event | category | flops | bytes accessed | tf_op | source)
XLA Modules:
  0.0 214.8 jit_solution(3780529455137462611)
XLA Ops:
  7.2 0.7 all-gather.2.cloned.1.call-update
  8.0 0.7 compare_select_fusion
  8.6 0.7 compare_and_fusion
  9.3 0.7 convert_multiply_fusion.1
  9.9 0.7 broadcast_compare_fusion
  10.7 1.0 fusion.21
  11.7 0.2 multiply_sine_fusion.1
  11.9 7.0 %gather_fusion = bf16[16,4096,64]{1,2,0:T(8,128)(2,1)} fusion(bf16[8,4096,64]{1,2,0:T(8,128)(2,1)} %param.17, s32[1024]{0:T(1024)S(1)} %pad_clamp_fusion), kind=kCustom, calls=%fused_computation | custom fusion | bytes 16777280 | tf_op jit(solution)/shard_map/jit(_take)/gather | solution.py:25
  18.9 6.9 %multiply_convert_fusion = bf16[512,4096]{1,0:T(8,128)(2,1)} fusion(bf16[512,4096]{1,0:T(8,128)(2,1)} %param.10, f32[16,4096]{1,0:T(8,128)S(1)} %copy-done, s32[512]{0:T(512)S(1)} %copy-done.2), kind=kOutput, calls=%fused_computation.13 | convolution fusion | flops 408952832 | bytes 8652800 | tf_op jit(solution)/shard_map/dot_general | solution.py:91
  25.9 11.8 %fusion.3 = (bf16[4096,16,64]{0,2,1:T(8,128)(2,1)}, bf16[4096,16,64]{0,2,1:T(8,128)(2,1)}, bf16[4096,16,64]{0,2,1:T(8,128)(2,1)}) fusion(f32[4096,16]{0,1:T(8,128)S(1)} %get-tuple-element.8, bf16[16,4096,64]{1,2,0:T(8,128)(2,1)} %gather_fusion, pred[16]{0:T(512)(128)(4,1)S(1)} %compare_and_fusion, f32[4096,16]{0,1:T(8,128)S(1)} %get-tuple-element.9, ...), kind=kLoop, calls=%fused_computation.10 | loop fusion | flops 33554432 | bytes 34340880 | tf_op jit(solution)/shard_map/convert.9
  37.6 25.2 %pad_maximum_fusion.3 = (bf16[4096,16,128]{0,2,1:T(8,128)(2,1)}, bf16[4096,16,128]{0,2,1:T(8,128)(2,1)}) fusion(bf16[4096,16,64]{0,2,1:T(8,128)(2,1)} %get-tuple-element.3, bf16[4096,16,64]{0,2,1:T(8,128)(2,1)} %get-tuple-element.5, bf16[4096,16,64]{0,2,1:T(8,128)(2,1)} %get-tuple-element.4), kind=kLoop, calls=%fused_computation.4 | loop fusion | flops 67108864 | bytes 58720256 | tf_op jit(solution)/shard_map/concatenate | solution.py:32
  62.9 2.9 %copy.17 = bf16[16,8,2,4096]{3,1,2,0:T(8,128)(2,1)S(1)} copy(bf16[16,8,2,4096]{3,2,1,0:T(2,128)(2,1)} %bitcast.55) | data formatting | bytes 4194304
  65.8 14.6 %fusion.7 = bf16[128,2048]{0,1:T(8,128)(2,1)S(1)} fusion(bf16[128,8192]{1,0:T(8,128)(2,1)S(1)} %bitcast.56, bf16[4096,2048]{0,1:T(8,128)(2,1)} %bitcast.52, bf16[4096,2048]{0,1:T(8,128)(2,1)} %bitcast.50), kind=kOutput, calls=%fused_computation.18 | convolution fusion | flops 4362338304 | bytes 36175872 | tf_op jit(solution)/shard_map/dot_general | solution.py:41
  80.4 0.2 copy.13
  80.8 0.1 copy.14
  80.9 0.4 convolution_convert_fusion.1
  81.3 0.7 reshape.165
  82.0 1.7 fusion.8
  83.8 3.7 %fusion.35 = f32[512,128]{0,1:T(8,128)S(1)} fusion(bf16[512,4096]{1,0:T(8,128)(2,1)} %multiply_convert_fusion, bf16[128,4096]{1,0:T(8,128)(2,1)S(1)} %reshape.165), kind=kOutput, calls=%fused_computation.67 | convolution fusion | flops 536870912 | bytes 5505024 | tf_op jit(solution)/shard_map/dot_general | solution.py:98
  87.5 0.4 fusion.34
  88.0 13.5 %pmax.7 = f32[512]{0:T(512)S(1)} all-reduce(f32[512]{0:T(512)S(1)} %get-tuple-element.14), channel_id=1, replica_groups=mesh['img'=8,'ori'=4] {'ori'}, use_global_device_ids=true, to_apply=%region_1.2 | all-reduce | flops 512 | bytes 4096 | tf_op jit(solution)/shard_map/pmax | solution.py:113
  101.5 15.5 %psum.14 = f32[512,8]{0,1:T(8,128)S(1)} all-reduce(f32[512,8]{0,1:T(8,128)S(1)} %bitcast_reduce_fusion), channel_id=1, replica_groups=mesh['img'=8,'ori'=4] {'ori'}, use_global_device_ids=true, to_apply=%region_3.4 | all-reduce | flops 4096 | bytes 32768 | tf_op jit(solution)/shard_map/psum | solution.py:116
  117.1 4.5 %convolution_convert_fusion = bf16[4096,128]{1,0:T(8,128)(2,1)} fusion(bf16[512,4096]{1,0:T(8,128)(2,1)} %multiply_convert_fusion, f32[512,128]{0,1:T(8,128)S(1)} %get-tuple-element.15, f32[512]{0:T(512)S(1)} %reduce_sum.19, f32[512]{0:T(512)S(1)} %pmax.7), kind=kOutput, calls=%fused_computation.15 | convolution fusion | flops 537591808 | bytes 5509120 | tf_op jit(solution)/shard_map/dot_general | solution.py:123
  121.6 34.6 %reduce-scatter.2.cloned.1.call-done = bf16[512,128]{1,0:T(8,128)(2,1)} async-done(((bf16[4096,128]{1,0:T(8,128)(2,1)}), bf16[512,128]{1,0:T(8,128)(2,1)}) %reduce-scatter.2.cloned.1.call-update) | async-done | bytes 131088 | tf_op jit(solution)/shard_map/reduce_scatter | solution.py:122
  156.3 1.0 copy.15
  157.3 0.2 convolution_convert_fusion.2
  157.5 12.1 %fusion.5 = bf16[16,8192]{1,0:T(8,128)(2,1)S(1)} fusion(bf16[4096,2048]{0,1:T(8,128)(2,1)} %bitcast.53, bf16[4096,2048]{0,1:T(8,128)(2,1)} %bitcast.51, bf16[2,8,16,128]{3,2,1,0:T(8,128)(2,1)S(1)} %bitcast.62), kind=kOutput, calls=%fused_computation.12 | convolution fusion | flops 604110848 | bytes 33882112 | tf_op jit(solution)/shard_map/dot_general | solution.py:67
  169.6 0.9 reshape.171
  170.5 0.6 log_add_fusion
  171.1 0.6 broadcast_divide_fusion
  171.7 34.5 %all-reduce.2.cloned.1.call-done = bf16[8,2,2,4096]{3,2,1,0:T(2,128)(2,1)} async-done(((bf16[8,2,2,4096]{3,2,1,0:T(2,128)(2,1)}), bf16[8,2,2,4096]{3,2,1,0:T(2,128)(2,1)}) %all-reduce.2.cloned.1.call-update) | async-done | bytes 262160 | tf_op jit(solution)/shard_map/psum | solution.py:132
  206.3 2.0 reshape.172
  (23 shorter events, 0.4 us)
Async XLA Ops:
  7.2 55.7 %all-gather.2.cloned.1.call-start = ((), (), s32[]{:S(2)}) async-start(), calls=%async_computation.1 | async-start | bytes 2359296 | tf_op jit(solution)/shard_map/all_gather | solution.py:95
  7.9 148.4 %reduce-scatter.2.cloned.1.call-start = ((), (), s32[]{:S(2)}) async-start(), calls=%async_computation.2 | async-start | bytes 1179648 | tf_op jit(solution)/shard_map/reduce_scatter | solution.py:122
  11.9 7.0 %copy-start = (f32[16,4096]{1,0:T(8,128)S(1)}, f32[16,4096]{1,0:T(8,128)}, u32[]{:S(2)}) copy-start(f32[16,4096]{1,0:T(8,128)} %param.15) | copy-start | bytes 786436
  11.9 7.0 %copy-start.2 = (s32[512]{0:T(512)S(1)}, s32[512]{0:T(512)}, u32[]{:S(2)}) copy-start(s32[512]{0:T(512)} %param.11) | copy-start | bytes 6148
  65.7 21.8 %copy-start.1 = (f32[512,8]{0,1:T(8,128)S(1)}, f32[512,8]{0,1:T(8,128)}, u32[]{:S(2)}) copy-start(f32[512,8]{0,1:T(8,128)} %param.14) | copy-start | bytes 49156
  65.8 21.8 %copy-start.3 = (f32[512]{0:T(512)S(1)}, f32[512]{0:T(512)}, u32[]{:S(2)}) copy-start(f32[512]{0:T(512)} %param.13) | copy-start | bytes 6148
  121.6 84.7 %all-reduce.2.cloned.1.call-start = ((), (), s32[]{:S(2)}) async-start(), calls=%async_computation.3 | async-start | bytes 524288 | tf_op jit(solution)/shard_map/psum | solution.py:132
Sparse Core Ops, SparseCore 0:
  9.9 30.4 all-gather.1
  121.7 34.5 reduce-scatter.1
  170.7 35.5 all-reduce.1
where the time goes:
time: 215 us
  waiting for transfers between devices  69.9 us (33%)
  matrix products  44.7 us (21%)
  other arithmetic  44.1 us (21%)
  blocking collectives  29 us (13%)
  between operations  13.9 us (6%)
  local copies, waits for them, and re-layouts  13 us (6%)
    reduce_scatter x1, waiting for transfers between devices, body(): lax.psum_scatter(lax.dot_general(part_img, weights, (((0,), (0,)), ((), (...  34.6 us
    psum x1, waiting for transfers between devices, body(): lax.psum(coef_own.astype(jnp.bfloat16), 'ori').astype(jnp.float32)  34.5 us
    concatenate x1, other arithmetic, rotated_ops(): upper = jnp.concatenate([cosine * chosen, -sine * chosen], axis=2)  25.2 us
    psum x1, blocking collectives, body(): totals = lax.psum(local_totals, 'ori')  15.5 us
    dot_general x1, matrix products, synthesize(): jnp.dot(flat_coef, rotator, preferred_element_type=jnp.float32)  14.6 us
    pmax x1, blocking collectives, body(): row_peak = lax.pmax(jnp.max(score, axis=1), 'ori')  13.5 us
    dot_general x1, matrix products, adjoint(): lax.dot_general(harmonics, rotator, (((1,), (1,)), ((), ())), preferred_e...  12.1 us
    another operation x1, other arithmetic  11.8 us
  transfers between devices with their start and end apart: 3, of which 2 were waited for; matrix products, arithmetic and copies ran while one was open for 26% of the time, Pallas kernels for 0%

commit v1 on v0

--- a/solution.py
+++ b/solution.py
@@ -81,6 +81,10 @@
     tilt_index,
     azimuth_index,
 ):
+
+    def roots_feed(view, mesh_dim="ori"):
+        return lax.all_gather(view, mesh_dim).sum(axis=0)
+
     angle_table = synth_table()
     image_rows = images.shape[0]
     classes = volume_coef.shape[0]
@@ -129,7 +133,7 @@
     )
     coef_own = adjoint(summed, rotator, angle_table, radial, classes)
     coef_sum = (
-        lax.psum(coef_own.astype(jnp.bfloat16), "ori")
+        roots_feed(coef_own.astype(jnp.bfloat16))
         .astype(jnp.float32)
         .reshape(classes, radial, 2, LM)
     )

time: 215 us -> 208 us (0.967)
  waiting for transfers between devices: 69.9 us -> 62.3 us
    psum x1 -> x0, waiting for transfers between devices: 34.5 us -> none  [body(): lax.psum(coef_own.astype(jnp.bfloat16), 'ori').astype(jnp.float32)]
    all_gather x0 -> x1, waiting for transfers between devices: none -> 26.9 us  [roots_feed(): return lax.all_gather(view, mesh_dim).sum(axis=0)]
  transfers between devices with their start and end apart: 3 -> 3, of which waited for: 2 -> 2; matrix products, arithmetic and copies ran while one was open for 26% -> 27% of each run, Pallas kernels for 0% -> 0%
where the time goes in v1:
time: 208 us
  waiting for transfers between devices  62.3 us (30%)
  matrix products  45.3 us (22%)
  other arithmetic  43.6 us (21%)
  blocking collectives  29 us (14%)
  between operations  13.9 us (7%)
  local copies, waits for them, and re-layouts  13.4 us (6%)
    reduce_scatter x1, waiting for transfers between devices, body(): lax.psum_scatter(lax.dot_general(part_img, weights, (((0,), (0,)), ((), (...  34.6 us
    all_gather x1, waiting for transfers between devices, roots_feed(): return lax.all_gather(view, mesh_dim).sum(axis=0)  26.9 us
    concatenate x1, other arithmetic, rotated_ops(): upper = jnp.concatenate([cosine * chosen, -sine * chosen], axis=2)  25.2 us
    psum x1, blocking collectives, body(): totals = lax.psum(local_totals, 'ori')  15.5 us
    dot_general x1, matrix products, synthesize(): jnp.dot(flat_coef, rotator, preferred_element_type=jnp.float32)  14.6 us
    pmax x1, blocking collectives, body(): row_peak = lax.pmax(jnp.max(score, axis=1), 'ori')  13.5 us
    dot_general x1, matrix products, adjoint(): lax.dot_general(harmonics, rotator, (((1,), (1,)), ((), ())), preferred_e...  12.8 us
    another operation x1, other arithmetic  11.8 us
  transfers between devices with their start and end apart: 3, of which 2 were waited for; matrix products, arithmetic and copies ran while one was open for 27% of the time, Pallas kernels for 0%

profile of v1, /device:TPU:0, one launch (start us, length us, event | category | flops | bytes accessed | tf_op | source)
XLA Modules:
  0.0 207.7 jit_solution(16149064580594544525)
XLA Ops:
  7.2 0.7 all-gather.4.cloned.1.call-update
  8.0 0.7 compare_select_fusion
  8.6 0.7 compare_and_fusion
  9.3 0.7 convert_multiply_fusion.1
  9.9 0.7 broadcast_compare_fusion
  10.7 1.0 fusion.21
  11.7 0.2 multiply_sine_fusion.1
  11.9 7.0 %gather_fusion = bf16[16,4096,64]{1,2,0:T(8,128)(2,1)} fusion(bf16[8,4096,64]{1,2,0:T(8,128)(2,1)} %param.17, s32[1024]{0:T(1024)S(1)} %pad_clamp_fusion), kind=kCustom, calls=%fused_computation | custom fusion | bytes 16777280 | tf_op jit(solution)/shard_map/jit(_take)/gather | solution.py:25
  18.9 6.9 %multiply_convert_fusion = bf16[512,4096]{1,0:T(8,128)(2,1)} fusion(bf16[512,4096]{1,0:T(8,128)(2,1)} %param.10, f32[16,4096]{1,0:T(8,128)S(1)} %copy-done, s32[512]{0:T(512)S(1)} %copy-done.2), kind=kOutput, calls=%fused_computation.13 | convolution fusion | flops 408952832 | bytes 8652800 | tf_op jit(solution)/shard_map/dot_general | solution.py:95
  25.9 11.8 %fusion.3 = (bf16[4096,16,64]{0,2,1:T(8,128)(2,1)}, bf16[4096,16,64]{0,2,1:T(8,128)(2,1)}, bf16[4096,16,64]{0,2,1:T(8,128)(2,1)}) fusion(f32[4096,16]{0,1:T(8,128)S(1)} %get-tuple-element.8, bf16[16,4096,64]{1,2,0:T(8,128)(2,1)} %gather_fusion, pred[16]{0:T(512)(128)(4,1)S(1)} %compare_and_fusion, f32[4096,16]{0,1:T(8,128)S(1)} %get-tuple-element.9, ...), kind=kLoop, calls=%fused_computation.10 | loop fusion | flops 33554432 | bytes 34340880 | tf_op jit(solution)/shard_map/convert.10
  37.6 25.2 %pad_maximum_fusion.3 = (bf16[4096,16,128]{0,2,1:T(8,128)(2,1)}, bf16[4096,16,128]{0,2,1:T(8,128)(2,1)}) fusion(bf16[4096,16,64]{0,2,1:T(8,128)(2,1)} %get-tuple-element.3, bf16[4096,16,64]{0,2,1:T(8,128)(2,1)} %get-tuple-element.5, bf16[4096,16,64]{0,2,1:T(8,128)(2,1)} %get-tuple-element.4), kind=kLoop, calls=%fused_computation.4 | loop fusion | flops 67108864 | bytes 58720256 | tf_op jit(solution)/shard_map/concatenate | solution.py:32
  62.9 2.9 %copy.17 = bf16[16,8,2,4096]{3,1,2,0:T(8,128)(2,1)S(1)} copy(bf16[16,8,2,4096]{3,2,1,0:T(2,128)(2,1)} %bitcast.56) | data formatting | bytes 4194304
  65.8 14.6 %fusion.7 = bf16[128,2048]{0,1:T(8,128)(2,1)S(1)} fusion(bf16[128,8192]{1,0:T(8,128)(2,1)S(1)} %bitcast.57, bf16[4096,2048]{0,1:T(8,128)(2,1)} %bitcast.53, bf16[4096,2048]{0,1:T(8,128)(2,1)} %bitcast.51), kind=kOutput, calls=%fused_computation.18 | convolution fusion | flops 4362338304 | bytes 36175872 | tf_op jit(solution)/shard_map/dot_general | solution.py:41
  80.4 0.2 copy.13
  80.8 0.1 copy.14
  80.9 0.4 convolution_convert_fusion.1
  81.3 0.7 reshape.163
  82.0 1.7 fusion.8
  83.8 3.7 %fusion.35 = f32[512,128]{0,1:T(8,128)S(1)} fusion(bf16[512,4096]{1,0:T(8,128)(2,1)} %multiply_convert_fusion, bf16[128,4096]{1,0:T(8,128)(2,1)S(1)} %reshape.163), kind=kOutput, calls=%fused_computation.67 | convolution fusion | flops 536870912 | bytes 5505024 | tf_op jit(solution)/shard_map/dot_general | solution.py:102
  87.5 0.4 fusion.34
  88.0 13.5 %pmax.7 = f32[512]{0:T(512)S(1)} all-reduce(f32[512]{0:T(512)S(1)} %get-tuple-element.14), channel_id=1, replica_groups=mesh['img'=8,'ori'=4] {'ori'}, use_global_device_ids=true, to_apply=%region_1.2 | all-reduce | flops 512 | bytes 4096 | tf_op jit(solution)/shard_map/pmax | solution.py:117
  101.5 15.5 %psum.7 = f32[512,8]{0,1:T(8,128)S(1)} all-reduce(f32[512,8]{0,1:T(8,128)S(1)} %bitcast_reduce_fusion), channel_id=1, replica_groups=mesh['img'=8,'ori'=4] {'ori'}, use_global_device_ids=true, to_apply=%region_3.4 | all-reduce | flops 4096 | bytes 32768 | tf_op jit(solution)/shard_map/psum | solution.py:120
  117.1 4.5 %convolution_convert_fusion = bf16[4096,128]{1,0:T(8,128)(2,1)} fusion(bf16[512,4096]{1,0:T(8,128)(2,1)} %multiply_convert_fusion, f32[512,128]{0,1:T(8,128)S(1)} %get-tuple-element.15, f32[512]{0:T(512)S(1)} %reduce_sum.31, f32[512]{0:T(512)S(1)} %pmax.7), kind=kOutput, calls=%fused_computation.15 | convolution fusion | flops 537591808 | bytes 5509120 | tf_op jit(solution)/shard_map/dot_general | solution.py:127
  121.6 34.6 %reduce-scatter.2.cloned.1.call-done = bf16[512,128]{1,0:T(8,128)(2,1)} async-done(((bf16[4096,128]{1,0:T(8,128)(2,1)}), bf16[512,128]{1,0:T(8,128)(2,1)}) %reduce-scatter.2.cloned.1.call-update) | async-done | bytes 131088 | tf_op jit(solution)/shard_map/reduce_scatter | solution.py:126
  156.3 1.0 copy.15
  157.3 0.2 convolution_convert_fusion.2
  157.5 12.8 %fusion.5 = bf16[16,8192]{1,0:T(8,128)(2,1)} fusion(bf16[4096,2048]{0,1:T(8,128)(2,1)} %bitcast.54, bf16[4096,2048]{0,1:T(8,128)(2,1)} %bitcast.52, bf16[2,8,16,128]{3,2,1,0:T(8,128)(2,1)S(1)} %bitcast.64), kind=kOutput, calls=%fused_computation.12 | convolution fusion | flops 604110848 | bytes 33882112 | tf_op jit(solution)/shard_map/dot_general | solution.py:67
  170.3 0.6 log_add_fusion
  170.9 0.6 broadcast_divide_fusion
  171.5 26.9 %all-gather.6.cloned.1.call-done = bf16[64,8192]{1,0:T(8,128)(2,1)} async-done(((bf16[16,8192]{1,0:T(8,128)(2,1)}), bf16[64,8192]{1,0:T(8,128)(2,1)}) %all-gather.6.cloned.1.call-update) | async-done | bytes 1048592 | tf_op jit(solution)/shard_map/all_gather | solution.py:86
  198.5 1.5 reduce_sum.32
  199.9 1.3 reshape.169
  (23 shorter events, 0.4 us)
Async XLA Ops:
  7.2 55.7 %all-gather.4.cloned.1.call-start = ((), (), s32[]{:S(2)}) async-start(), calls=%async_computation.1 | async-start | bytes 2359296 | tf_op jit(solution)/shard_map/all_gather | solution.py:99
  7.9 148.4 %reduce-scatter.2.cloned.1.call-start = ((), (), s32[]{:S(2)}) async-start(), calls=%async_computation.2 | async-start | bytes 1179648 | tf_op jit(solution)/shard_map/reduce_scatter | solution.py:126
  11.9 7.0 %copy-start = (f32[16,4096]{1,0:T(8,128)S(1)}, f32[16,4096]{1,0:T(8,128)}, u32[]{:S(2)}) copy-start(f32[16,4096]{1,0:T(8,128)} %param.15) | copy-start | bytes 786436
  11.9 7.0 %copy-start.2 = (s32[512]{0:T(512)S(1)}, s32[512]{0:T(512)}, u32[]{:S(2)}) copy-start(s32[512]{0:T(512)} %param.11) | copy-start | bytes 6148
  65.7 21.8 %copy-start.1 = (f32[512,8]{0,1:T(8,128)S(1)}, f32[512,8]{0,1:T(8,128)}, u32[]{:S(2)}) copy-start(f32[512,8]{0,1:T(8,128)} %param.14) | copy-start | bytes 49156
  65.8 21.8 %copy-start.3 = (f32[512]{0:T(512)S(1)}, f32[512]{0:T(512)}, u32[]{:S(2)}) copy-start(f32[512]{0:T(512)} %param.13) | copy-start | bytes 6148
  121.6 76.9 %all-gather.6.cloned.1.call-start = ((), (), s32[]{:S(2)}) async-start(), calls=%async_computation.3 | async-start | bytes 1310720 | tf_op jit(solution)/shard_map/all_gather | solution.py:86
Sparse Core Ops, SparseCore 0:
  9.9 30.4 all-gather.3
  121.7 34.5 reduce-scatter.1
  170.4 27.9 all-gather.5
